TPU v7x, 32 devices: a whole 2x2x4 slice. The times are simulated.
32 devices in a mesh: row: 2 (over x), col: 4 (over y, core), layer: 4 (over z).
Axes of the slice: x: 2, y: 2, z: 4, core: 2. Of those that a mesh axis runs over, the one named last changes fastest.
Arguments:
- a_cyclic: float32 [4, 1024, 4096], P('layer', 'row', 'col'), may hold values from -6 to 6
- a_mask: int32 [4, 8, 32], P('layer', 'row', 'col'), may hold values from 0 to 1, as said below
- b_dense: float32 [16384, 16384], P('row', ('col', 'layer')), may hold values from -0.21875 to 0.21875
- b_mask: int32 [128, 128], P('row', ('col', 'layer')), may hold values from 0 to 1, as said below
Outputs:
- product: float32 [1024, 16384], P('row', ('col', 'layer'))
Inputs may be any that keep to these rules, and one draw needn't show every extreme that they name: For each l, each run of 4 block rows starting at a multiple of 4 and each run of 8 block columns starting at a multiple of 8, those blocks of a_mask[l] hold 1 to 12 ones. In every draw, for some l and some row run, the groups of all 4 column runs hold exactly 12. `b_mask`: take the block rows r * 64 to (r + 1) * 64 - 1, a residue d modulo 4, and the block columns g * 8 to (g + 1) * 8 - 1: the blocks among them whose row index is d modulo 4 hold 1 to 48 ones. In every draw, for some r, d and c, the groups of all g from c * 4 to c * 4 + 3 hold exactly 48.
All inputs are finite; a program needn't handle non-finite values.
Results may differ from a plain program's by a relative error of at most 0.00007.
Values sent between devices are 32-bit elements; how exact they have to be, the bound alone decides.
A program may use at most 256 MiB of HBM per device.

v0:
```python
import jax
import jax.numpy as jnp
from jax import lax
from jax.sharding import PartitionSpec as P

precise = lax.Precision.HIGHEST


def to_blocks(matrix, block_size):
    row_blocks = matrix.shape[0] // block_size
    col_blocks = matrix.shape[1] // block_size
    shaped = matrix.reshape(row_blocks, block_size, col_blocks, block_size).transpose(0, 2, 1, 3)
    return shaped.reshape(row_blocks * col_blocks, block_size, block_size)


def pack_blocks(blocks, is_live, capacity):
    total_places = is_live.shape[0]
    rank_of = jnp.cumsum(is_live) - 1
    slot_numbers = jnp.arange(capacity, dtype=jnp.int32)
    chosen = (is_live[None, :] > 0) & (rank_of[None, :] == slot_numbers[:, None])
    weights = chosen.astype(jnp.float32)
    packed = jnp.einsum("cg,gxy->cxy", weights, blocks, precision=precise)
    places = jnp.arange(total_places, dtype=jnp.int32)
    any_match = jnp.any(chosen, axis=1)
    position = jnp.sum(jnp.where(chosen, places[None, :], 0), axis=1)
    slot_ids = jnp.where(any_match, position, -1)
    return (packed, slot_ids)


def lookup_table(gathered, key_of, key_count):
    slot_count = gathered.shape[0]
    key_values = jnp.arange(key_count, dtype=jnp.int32)
    matches = key_of[:, None] == key_values[None, :]
    any_match = jnp.any(matches, axis=0)
    slot_numbers = jnp.arange(slot_count, dtype=jnp.int32)
    slot_index = jnp.sum(jnp.where(matches, slot_numbers[:, None], 0), axis=0)
    slot_of = jnp.where(any_match, slot_index, slot_count)
    padded = jnp.concatenate([gathered, jnp.zeros((1,) + gathered.shape[1:], jnp.float32)], axis=0)
    return (padded, slot_of)


def accumulate(running, slot_data, slot_ids, source, padded, slot_of, k_step, jwidth):
    row_blocks = running.shape[0]
    is_live = slot_ids >= 0
    clipped = jnp.maximum(slot_ids, 0)
    k_index = source * k_step + clipped // jwidth
    column = clipped % jwidth
    rows_here = jnp.arange(row_blocks, dtype=jnp.int32)
    where_rows = slot_of[k_index[:, None] * row_blocks + rows_here[None, :]]
    a_pieces = padded[where_rows]
    b_pieces = jnp.where(is_live[:, None, None], slot_data, 0.0)
    products = jnp.einsum("smxa,sab->smxb", a_pieces, b_pieces, precision=precise)
    spread = (
        (column[:, None] == jnp.arange(jwidth, dtype=jnp.int32)[None, :]) & is_live[:, None]
    ).astype(jnp.float32)
    return running + jnp.einsum("smxb,sj->mxjb", products, spread, precision=precise)


def make_folder(padded, slot_of, k_step, jwidth, shard):

    def fold_piece(running, portion, offset):
        slot_data, slot_ids = portion
        sources = slot_data.shape[0] // shard
        slot_groups = slot_data.reshape((sources, shard) + slot_data.shape[1:])
        id_groups = slot_ids.reshape(sources, shard)
        source_rows = jnp.arange(sources, dtype=jnp.int32)

        def add_source(carry, inputs):
            group_slots, group_ids, source = inputs
            return (
                accumulate(carry, group_slots, group_ids, source, padded, slot_of, k_step, jwidth),
                None,
            )

        result, unused = lax.scan(add_source, running, (slot_groups, id_groups, source_rows))
        return result

    return fold_piece


def on_device(a_cyclic, a_mask, b_dense, b_mask):
    block_size = a_cyclic.shape[1] // a_mask.shape[1]
    layer_count = lax.axis_size("layer")
    row_count = lax.axis_size("row")
    row_blocks = a_mask.shape[1]
    q_blocks = a_mask.shape[2]
    k_run = b_mask.shape[0]
    j_run = b_mask.shape[1]
    per_layer = k_run // layer_count
    a_capacity = max(2, row_blocks * q_blocks * 3 // 8)
    b_capacity = max(2, per_layer * j_run * 3 // 8)
    a_blocks = to_blocks(a_cyclic[0], block_size)
    a_slots, a_ids = pack_blocks(a_blocks, a_mask[0].reshape(-1), a_capacity)
    b_blocks = to_blocks(b_dense, block_size)
    gathered, gathered_ids = (
        lax.all_gather(a_slots, ("col", "layer"), axis=0, tiled=True),
        lax.all_gather(a_ids, ("col", "layer"), axis=0, tiled=True),
    )
    from_device = jnp.arange(gathered.shape[0], dtype=jnp.int32) // a_capacity
    from_col = from_device // layer_count
    from_layer = from_device % layer_count
    clipped = jnp.maximum(gathered_ids, 0)
    k_index = (from_col * q_blocks + clipped % q_blocks) * layer_count + from_layer
    key_of = jnp.where(gathered_ids >= 0, k_index * row_blocks + clipped // q_blocks, -1)
    padded, slot_of = lookup_table(gathered, key_of, k_run * row_count * row_blocks)
    b_slots, b_ids = pack_blocks(b_blocks, b_mask.reshape(-1), layer_count * b_capacity)
    zero_sum = jnp.zeros((row_blocks, block_size, j_run, block_size), jnp.float32)
    folder = make_folder(padded, slot_of, k_run, j_run, layer_count * b_capacity)
    running = folder(
        zero_sum,
        (
            lax.all_gather(b_slots, "row", axis=0, tiled=True),
            lax.all_gather(b_ids, "row", axis=0, tiled=True),
        ),
        jnp.int32(0),
    )
    return running.reshape(row_blocks * block_size, j_run * block_size)


def solution(mesh):
    placed = (
        P("layer", "row", "col"),
        P("layer", "row", "col"),
        P("row", ("col", "layer")),
        P("row", ("col", "layer")),
    )
    return jax.shard_map(
        on_device, mesh=mesh, in_specs=placed, out_specs=P("row", ("col", "layer")), check_vma=False
    )
```

profile of v0, /device:TPU:0, one launch (start us, length us, event | category | flops | bytes accessed | tf_op | source)
XLA Modules:
  0.0 719.3 jit_solution(1314038571946012761)
XLA Ops:
  6.5 0.8 reshape.258
  7.3 0.7 broadcast_compare_fusion.2
  8.0 0.1 add_reduce_fusion
  8.2 2.1 copy.28
  10.3 0.8 fusion.21
  11.2 1.1 copy.22
  12.4 0.8 copy.19
  13.2 0.3 reduce-window.19
  13.6 0.7 broadcast_compare_fusion.1
  14.3 0.1 copy.18
  14.5 27.6 %copy.29 = f32[1024,8,8,128]{3,2,1,0:T(8,128)} copy(f32[1024,8,8,128]{3,1,2,0:T(8,128)} %bitcast.104) | data formatting | bytes 67108864
  42.2 0.1 slice_reduce_fusion
  42.4 25.7 %fusion.18 = f32[192,128,128]{2,0,1:T(8,128)} fusion(s32[512]{0:T(512)S(1)} %add_bitcast_fusion, pred[512]{0:T(512)(128)(4,1)S(1)} %gt.30, f32[64,128,8,128]{3,2,1,0:T(8,128)} %bitcast.101), kind=kOutput, calls=%fused_computation.34 | convolution fusion | flops 19327549440 | bytes 46139904 | tf_op jit(solution)/shard_map/cg,gxy->cxy/dot_general | solution.py:22
  68.1 0.6 copy-done.1
  68.7 0.6 dynamic-slice.1
  69.3 0.6 dynamic-slice
  70.5 0.1 fusion.27
  70.6 0.2 select_reduce_fusion.1
  70.8 0.1 select_dynamic-update-slice_fusion
  70.9 4.7 all-reduce.1
  76.3 0.1 fusion.33
  76.4 0.1 select_reduce_fusion.2
  76.6 12.7 %all-reduce.2 = s32[192]{0:T(256)S(1)} all-reduce(s32[192]{0:T(256)S(1)} %select_dynamic-update-slice_fusion.1), channel_id=1, replica_groups=mesh['row'=2,'col'=4,'layer'=4] {'col','layer'}, use_global_device_ids=true, to_apply=%add.2 | all-reduce | flops 192 | bytes 1536
  89.4 0.1 fusion.24
  89.5 0.1 select_reduce_fusion
  89.7 26.1 %all-gather.3.cloned.1.call-done = f32[192,128,128]{2,1,0:T(8,128)} async-done(((f32[12,128,128]{2,1,0:T(8,128)}), f32[192,128,128]{2,1,0:T(8,128)}) %all-gather.3.cloned.1.call-update) | async-done | bytes 12582928 | tf_op jit(solution)/shard_map/all_gather | solution.py:96
  115.7 15.9 %concatenate.3 = f32[193,128,128]{2,1,0:T(8,128)} pad(f32[192,128,128]{2,1,0:T(8,128)} %all-gather.3.cloned.1.call-done, f32[]{:T(128)} %constant.149.clone.1), padding=0_1x0_0x0_0 | pad | bytes 25231364 | tf_op jit(solution)/shard_map/concatenate | solution.py:38
  131.6 279.9 %all-gather.5.cloned.1.call-done = f32[384,128,128]{2,0,1:T(8,128)} async-done(((f32[192,128,128]{2,0,1:T(8,128)}), f32[384,128,128]{2,0,1:T(8,128)}) %all-gather.5.cloned.1.call-update) | async-done | bytes 25165840 | tf_op jit(solution)/shard_map/all_gather | solution.py:112
  411.5 299.1 %while.13 = (s32[]{:T(128)}, f32[4,128,8,128]{3,2,1,0:T(8,128)S(1)}, s32[2,192]{1,0:T(2,128)S(1)}, s32[2]{0:T(128)S(1)}, s32[512]{0:T(512)S(1)}, /*index=5*/f32[...) while((s32[]{:T(128)}, ...), condition=%wide.region_10.11_spmd.clone, body=%wide.region_9.10_spmd.clone.sunk | while | flops 20539518976 | bytes 293664320 | solution.py:75
  411.6 0.6 dynamic_slice.43
  412.9 0.1 reshape.273
  413.1 5.0 gather_fusion
  418.1 0.1 gather.26
  418.2 0.1 reshape.274
  418.3 26.8 %gather_fusion.1 = f32[768,128,128]{2,1,0:T(8,128)} fusion(f32[193,128,128]{2,1,0:T(8,128)} %get-tuple-element.243, s32[1024]{0:T(1024)S(1)} %pad_clamp_fusion.5), kind=kCustom, calls=%fused_computation.1.clone.clone.1 | custom fusion | bytes 100666368 | tf_op jit(solution)/shard_map/while/body/eval_jaxpr/gather | solution.py:50
  445.1 10.7 %constant_dynamic-slice_fusion.3 = f32[1,192,128,128]{3,1,0,2:T(8,128)} fusion(f32[2,192,128,128]{3,1,0,2:T(8,128)} %get-tuple-element.244, s32[]{:T(128)} %get-tuple-element.228), kind=kLoop, calls=%fused_computation.30.clone.1 | loop fusion | bytes 25165828 | tf_op jit(solution)/shard_map/while/body/jit(dynamic_index_in_dim)/dynamic_slice | solution.py:75
  455.8 52.8 %fusion.53 = f32[192,4,128,128]{3,2,1,0:T(8,128)} fusion(f32[192,4,128,128]{3,2,1,0:T(8,128)} %bitcast.100, f32[1,192,128,128]{3,1,0,2:T(8,128)} %constant_dynamic-slice_fusion.3, pred[192]{0:T(512)(128)(4,1)S(1)} %get-tuple-element.216), kind=kOutput, calls=%fused_computation.7.clone.2 | convolution fusion | flops 19330498560 | bytes 113246400 | tf_op jit(solution)/shard_map/while/body/eval_jaxpr/smxa,sab->smxb/dot_general | solution.py:52
  508.6 52.5 %bitcast_add_fusion.2 = f32[4,128,8,128]{3,2,1,0:T(8,128)S(1)} fusion(f32[4,128,8,128]{3,2,1,0:T(8,128)S(1)} %get-tuple-element.229, f32[192,4,128,128]{3,2,1,0:T(8,128)} %fusion.53, pred[]{:T(512)S(6)} %compare.15, s32[192]{0:T(256)S(1)} %get-tuple-element.217, pred[192]{0:T(512)(128)(4,1)S(1)} %get-tuple-element.216), kind=kOutput, calls=%fused_computation.10.clone.1 | convolution fusion | flops 1209011200 | bytes 54526912 | tf_op jit(solution)/shard_map/while/body/eval_jaxpr/smxb,sj->mxjb/dot_general | solution.py:56
  561.3 0.6 dynamic_slice.43
  562.6 0.1 reshape.273
  562.7 5.0 gather_fusion
  567.8 0.1 gather.26
  567.9 0.1 reshape.274
  568.0 26.5 %gather_fusion.1 = f32[768,128,128]{2,1,0:T(8,128)} fusion(f32[193,128,128]{2,1,0:T(8,128)} %get-tuple-element.243, s32[1024]{0:T(1024)S(1)} %pad_clamp_fusion.5), kind=kCustom, calls=%fused_computation.1.clone.clone.1 | custom fusion | bytes 100666368 | tf_op jit(solution)/shard_map/while/body/eval_jaxpr/gather | solution.py:50
  594.6 10.7 %constant_dynamic-slice_fusion.3 = f32[1,192,128,128]{3,1,0,2:T(8,128)} fusion(f32[2,192,128,128]{3,1,0,2:T(8,128)} %get-tuple-element.244, s32[]{:T(128)} %get-tuple-element.228), kind=kLoop, calls=%fused_computation.30.clone.1 | loop fusion | bytes 25165828 | tf_op jit(solution)/shard_map/while/body/jit(dynamic_index_in_dim)/dynamic_slice | solution.py:75
  605.3 52.8 %fusion.53 = f32[192,4,128,128]{3,2,1,0:T(8,128)} fusion(f32[192,4,128,128]{3,2,1,0:T(8,128)} %bitcast.100, f32[1,192,128,128]{3,1,0,2:T(8,128)} %constant_dynamic-slice_fusion.3, pred[192]{0:T(512)(128)(4,1)S(1)} %get-tuple-element.216), kind=kOutput, calls=%fused_computation.7.clone.2 | convolution fusion | flops 19330498560 | bytes 113246400 | tf_op jit(solution)/shard_map/while/body/eval_jaxpr/smxa,sab->smxb/dot_general | solution.py:52
  658.1 52.5 %bitcast_add_fusion.2 = f32[4,128,8,128]{3,2,1,0:T(8,128)S(1)} fusion(f32[4,128,8,128]{3,2,1,0:T(8,128)S(1)} %get-tuple-element.229, f32[192,4,128,128]{3,2,1,0:T(8,128)} %fusion.53, pred[]{:T(512)S(6)} %compare.15, s32[192]{0:T(256)S(1)} %get-tuple-element.217, pred[192]{0:T(512)(128)(4,1)S(1)} %get-tuple-element.216), kind=kOutput, calls=%fused_computation.10.clone.1 | convolution fusion | flops 1209011200 | bytes 54526912 | tf_op jit(solution)/shard_map/while/body/eval_jaxpr/smxb,sj->mxjb/dot_general | solution.py:56
  710.7 1.8 copy.52
  (36 shorter events, 1.2 us)
Async XLA Ops:
  6.5 109.2 %all-gather.3.cloned.1.call-start = ((), (), s32[]{:S(2)}) async-start(), calls=%async_computation | async-start | bytes 13369344 | tf_op jit(solution)/shard_map/all_gather | solution.py:96
  12.3 399.2 %all-gather.5.cloned.1.call-start = ((), (), s32[]{:S(2)}) async-start(), calls=%async_computation.1 | async-start | bytes 37748736 | tf_op jit(solution)/shard_map/all_gather | solution.py:112
  68.0 0.7 copy-start.1
  68.0 1.3 copy-start
Sparse Core Ops, SparseCore 0:
  12.4 103.2 all-gather.2
  117.3 294.2 all-gather.4
where the time goes:
time: 720 us; the launch traced here: 719 us
  waiting for transfers between devices  306 us (42%)
  matrix products  237 us (33%)
  local copies, waits for them, and re-layouts  139 us (19%)
  blocking collectives  17.4 us (2%)
  between operations  14.7 us (2%)
    all_gather x1, waiting for transfers between devices, on_device(): lax.all_gather(b_slots, 'row', axis=0, tiled=True)  280 us
    dot_general x2, matrix products, accumulate(): jnp.einsum('smxa,sab->smxb', a_pieces, b_pieces, precision=precise)  106 us
    dot_general x2, matrix products, accumulate(): jnp.einsum('smxb,sj->mxjb', products, spread, precision=precise)  105 us
    gather x2, local copies, waits for them, and re-layouts, accumulate(): a_pieces = padded[where_rows]  53.3 us
    unnamed x12, local copies, waits for them, and re-layouts  34.1 us
    dot_general x2, matrix products, pack_blocks(): packed = jnp.einsum('cg,gxy->cxy', weights, blocks, precision=precise)  26.5 us
    all_gather x1, waiting for transfers between devices, on_device(): lax.all_gather(a_slots, ('col', 'layer'), axis=0, tiled=True)  26.1 us
    dynamic_slice x4, local copies, waits for them, and re-layouts, fold_piece(): lax.scan(add_source, running, (slot_groups, id_groups, source_rows))  22.6 us
  transfers between devices with their start and end apart: 2, of which 2 were waited for; matrix products, arithmetic and copies ran while one was open for 10% of the time, Pallas kernels for 0%

commit v1 on v0

--- a/solution.py
+++ b/solution.py
@@ -1,6 +1,10 @@
+import functools
+
 import jax
 import jax.numpy as jnp
 from jax import lax
+from jax.experimental import pallas as pl
+from jax.experimental.pallas import tpu as pltpu
 from jax.sharding import PartitionSpec as P
 
 precise = lax.Precision.HIGHEST
@@ -117,6 +121,187 @@
     return running.reshape(row_blocks * block_size, j_run * block_size)
 
 
+CHUNK = 2
+DEPTH = 4
+MASK_ROWS = 8
+
+
+def pack_kernel(block_size, capacity, places, mask_ref, a_ref, out_ref, sems):
+    copies = []
+    for slot in range(capacity):
+        row = pl.multiple_of(places[0, slot] * block_size, block_size)
+        column = pl.multiple_of(places[1, slot] * block_size, block_size)
+        copies.append(
+            pltpu.make_async_copy(
+                a_ref.at[pl.ds(row, block_size), pl.ds(column, block_size)],
+                out_ref.at[pl.ds(slot * block_size, block_size), :],
+                sems.at[slot],
+            )
+        )
+    for copy in copies:
+        copy.start()
+    out_ref[pl.ds(capacity * block_size, MASK_ROWS), :] = mask_ref[...]
+    for copy in copies:
+        copy.wait()
+
+
+def pack_a(a_local, mask, block_size, capacity):
+    row_blocks, q_blocks = mask.shape
+    flat = mask.reshape(-1)
+    spots = row_blocks * q_blocks
+    order = jnp.arange(spots, dtype=jnp.int32)
+    before = jnp.sum(jnp.where(order[None, :] < order[:, None], flat[None, :], 0), axis=1)
+    slots = jnp.arange(capacity, dtype=jnp.int32)
+    chosen = (flat[None, :] > 0) & (before[None, :] == slots[:, None])
+    position = jnp.sum(jnp.where(chosen, order[None, :], 0), axis=1)
+    places = jnp.stack([position // q_blocks, position % q_blocks])
+    mask_rows = jnp.zeros((MASK_ROWS, block_size), jnp.float32)
+    mask_rows = mask_rows.at[0, :spots].set(flat.astype(jnp.float32))
+    return pl.pallas_call(
+        functools.partial(pack_kernel, block_size, capacity),
+        out_shape=jax.ShapeDtypeStruct((capacity * block_size + MASK_ROWS, block_size), jnp.float32),
+        in_specs=[
+            pl.BlockSpec(memory_space=pltpu.SMEM),
+            pl.BlockSpec(memory_space=pltpu.VMEM),
+            pl.BlockSpec(memory_space=pl.ANY),
+        ],
+        out_specs=pl.BlockSpec(memory_space=pltpu.VMEM),
+        scratch_shapes=[pltpu.SemaphoreType.DMA((capacity,))],
+    )(places, mask_rows, a_local)
+
+
+def split(value):
+    high = value.astype(jnp.bfloat16)
+    low = (value - high.astype(jnp.float32)).astype(jnp.bfloat16)
+    return high, low
+
+
+def product_kernel(
+    block_size, all_rows, k_run, table, scale_ref, a_ref, b_ref, theirs_ref, mine_ref,
+    total, tile, high_ref, low_ref, offset_of, row_of, sems
+):
+    def fetch(k):
+        slot = lax.rem(k, DEPTH)
+        row = pl.multiple_of(k * block_size, block_size)
+        return pltpu.make_async_copy(
+            b_ref.at[pl.ds(row, block_size), :], tile.at[slot], sems.at[slot]
+        )
+
+    for k in range(DEPTH - 1):
+        fetch(k).start()
+    total[...] = jnp.zeros_like(total)
+
+    @pl.loop(0, k_run)
+    def step(k):
+        @pl.when(k + DEPTH - 1 < k_run)
+        def ahead():
+            fetch(k + DEPTH - 1).start()
+
+        count = jnp.int32(0)
+        for m in range(all_rows):
+            offset = table[k * all_rows + m]
+            offset_of[count] = offset
+            row_of[count] = m
+            count = count + (offset >= 0).astype(jnp.int32)
+        for extra in range(CHUNK - 1):
+            offset_of[count + extra] = 0
+            row_of[count + extra] = all_rows
+        fetch(k).wait()
+
+        @pl.when(count > 0)
+        def used():
+            slot = lax.rem(k, DEPTH)
+            high, low = split(tile[slot] * scale_ref[pl.ds(k, 1), :])
+            high_ref[pl.ds(0, block_size), :] = high
+            high_ref[pl.ds(block_size, block_size), :] = high
+            low_ref[pl.ds(0, block_size), :] = low
+            low_ref[pl.ds(block_size, block_size), :] = low
+
+            @pl.loop(0, (count + CHUNK - 1) // CHUNK)
+            def chunk(c):
+                pieces = []
+                for i in range(CHUNK):
+                    start = pl.multiple_of(offset_of[c * CHUNK + i], MASK_ROWS)
+                    a_high, a_low = split(a_ref[pl.ds(start, block_size), :])
+                    pieces.append(jnp.concatenate([a_high, a_low], axis=1))
+                left = jnp.concatenate(pieces, axis=0)
+                part = jnp.dot(left, high_ref[...], preferred_element_type=jnp.float32)
+                part = part + jnp.dot(left, low_ref[...], preferred_element_type=jnp.float32)
+                for i in range(CHUNK):
+                    row = pl.multiple_of(row_of[c * CHUNK + i] * block_size, block_size)
+                    total[pl.ds(row, block_size), :] += part[i * block_size:(i + 1) * block_size]
+
+    half = theirs_ref.shape[0]
+    theirs_ref[...] = total[pl.ds(0, half), :]
+    mine_ref[...] = total[pl.ds(half, half), :]
+
+
+def multiply(table, scale, gathered, b_local, block_size, all_rows):
+    k_size, width = b_local.shape
+    k_run = k_size // block_size
+    half = all_rows // 2 * block_size
+    result = jax.ShapeDtypeStruct((half, width), jnp.float32)
+    vmem = pl.BlockSpec(memory_space=pltpu.VMEM)
+    return pl.pallas_call(
+        functools.partial(product_kernel, block_size, all_rows, k_run),
+        out_shape=(result, result),
+        in_specs=[
+            pl.BlockSpec(memory_space=pltpu.SMEM),
+            vmem,
+            vmem,
+            pl.BlockSpec(memory_space=pl.ANY),
+        ],
+        out_specs=(vmem, vmem),
+        scratch_shapes=[
+            pltpu.VMEM(((all_rows + 1) * block_size, width), jnp.float32),
+            pltpu.VMEM((DEPTH, block_size, width), jnp.float32),
+            pltpu.VMEM((2 * block_size, width), jnp.bfloat16),
+            pltpu.VMEM((2 * block_size, width), jnp.bfloat16),
+            pltpu.SMEM((all_rows + CHUNK,), jnp.int32),
+            pltpu.SMEM((all_rows + CHUNK,), jnp.int32),
+            pltpu.SemaphoreType.DMA((DEPTH,)),
+        ],
+        compiler_params=pltpu.CompilerParams(vmem_limit_bytes=60 * 1024 * 1024),
+    )(table, scale, gathered, b_local)
+
+
+def gather_a(payload, cols_per_row):
+    row_count, col_count = lax.axis_size("row"), lax.axis_size("col")
+    pairs = []
+    for row in range(row_count):
+        for col in range(col_count):
+            target = (col // cols_per_row) * col_count + row * cols_per_row + col % cols_per_row
+            pairs.append((row * col_count + col, target))
+    moved = lax.ppermute(payload, ("row", "col"), pairs)
+    return lax.all_gather(moved, ("col", "layer"), axis=0, tiled=True)
+
+
+def on_pair_device(a_cyclic, a_mask, b_dense, b_mask):
+    row_blocks, q_blocks = a_mask.shape[1:]
+    block_size = a_cyclic.shape[1] // row_blocks
+    layer_count, row_count = lax.axis_size("layer"), lax.axis_size("row")
+    cols_per_row = lax.axis_size("col") // row_count
+    capacity = max(2, row_blocks * q_blocks * 3 // 8)
+    all_rows = row_blocks * row_count
+    payload = pack_a(a_cyclic[0], a_mask[0], block_size, capacity)
+    gathered = gather_a(payload, cols_per_row)
+    spots = row_blocks * q_blocks
+    stride = payload.shape[0]
+    sources = gathered.shape[0] // stride
+    mask = gathered.reshape(sources, stride, block_size)[:, capacity * block_size, :spots]
+    order = jnp.arange(spots, dtype=jnp.int32)
+    earlier = order[None, :] < order[:, None]
+    rank = jnp.sum(jnp.where(earlier[None], mask[:, None, :], 0.0), axis=2).astype(jnp.int32)
+    first = jnp.arange(sources, dtype=jnp.int32)[:, None] * stride
+    offset = jnp.where(mask > 0, first + rank * block_size, -1)
+    offset = offset.reshape(row_count, cols_per_row, layer_count, row_blocks, q_blocks)
+    offset = offset.transpose(1, 4, 2, 0, 3)
+    offset = jnp.where(lax.axis_index("row") == 0, offset[:, :, :, ::-1], offset)
+    scale = jnp.repeat(b_mask.astype(jnp.float32), block_size, axis=1)
+    theirs, mine = multiply(offset.reshape(-1), scale, gathered, b_dense, block_size, all_rows)
+    return mine + lax.ppermute(theirs, "row", [(0, 1), (1, 0)])
+
+
 def solution(mesh):
     placed = (
         P("layer", "row", "col"),
@@ -124,6 +309,8 @@
         P("row", ("col", "layer")),
         P("row", ("col", "layer")),
     )
+    pair = mesh.shape["row"] == 2 and mesh.shape["col"] % 2 == 0
     return jax.shard_map(
-        on_device, mesh=mesh, in_specs=placed, out_specs=P("row", ("col", "layer")), check_vma=False
+        on_pair_device if pair else on_device,
+        mesh=mesh, in_specs=placed, out_specs=P("row", ("col", "layer")), check_vma=False,
     )

time: 720 us -> 253 us (0.35)
  matrix products: 237 us -> 0 us
  waiting for transfers between devices: 306 us -> 169 us
  local copies, waits for them, and re-layouts: 139 us -> 5.24 us
  Pallas kernels: 0 us -> 52 us
  blocking collectives: 17.4 us -> 0 us
  starting transfers between devices: 0.04 us -> 7.59 us
    dot_general x6 -> x0, matrix products: 237 us -> none  [the longest x2 106 us: accumulate(): jnp.einsum('smxa,sab->smxb', a_pieces, b_pieces, precision=precise)]
    all_gather x2 -> x1, waiting for transfers between devices: 306 us -> 122 us  [gather_a(): return lax.all_gather(moved, ('col', 'layer'), axis=0, tiled=True)]
    gather x6 -> x0, local copies, waits for them, and re-layouts: 63.6 us -> none  [the longest x2 53.3 us: accumulate(): a_pieces = padded[where_rows]]
    pallas_call x0 -> x2, Pallas kernels: none -> 52 us  [the longest x1 49.1 us: multiply(): pl.pallas_call(functools.partial(product_kernel, block_size, all_rows, k_...]
    ppermute x0 -> x2, waiting for transfers between devices: none -> 46.3 us  [the longest x1 46.3 us: on_pair_device(): return mine + lax.ppermute(theirs, 'row', [(0, 1), (1, 0)])]
    unnamed x12 -> x5, local copies, waits for them, and re-layouts: 34.1 us -> 1.67 us
    dynamic_slice x4 -> x0, local copies, waits for them, and re-layouts: 22.6 us -> none  [fold_piece(): lax.scan(add_source, running, (slot_groups, id_groups, source_rows))]
    unnamed x2 -> x0, blocking collectives: 17.4 us -> none
  transfers between devices with their start and end apart: 2 -> 3, of which waited for: 2 -> 2; matrix products, arithmetic and copies ran while one was open for 10% -> 0% of each run, Pallas kernels for 0% -> 0%
where the time goes in v1:
time: 253 us; the launch traced here: 252 us
  waiting for transfers between devices  169 us (67%)
  Pallas kernels  52 us (21%)
  between operations  13.5 us (5%)
  starting transfers between devices  7.59 us (3%)
  local copies, waits for them, and re-layouts  5.24 us (2%)
  other arithmetic  5.08 us (2%)
    all_gather x1, waiting for transfers between devices, gather_a(): return lax.all_gather(moved, ('col', 'layer'), axis=0, tiled=True)  122 us
    pallas_call x1, Pallas kernels, multiply(): pl.pallas_call(functools.partial(product_kernel, block_size, all_rows, k_...  49.1 us
    ppermute x1, waiting for transfers between devices, on_pair_device(): return mine + lax.ppermute(theirs, 'row', [(0, 1), (1, 0)])  46.3 us
    ppermute x1, starting transfers between devices, on_pair_device(): return mine + lax.ppermute(theirs, 'row', [(0, 1), (1, 0)])  5.8 us
  transfers between devices with their start and end apart: 3, of which 2 were waited for; matrix products, arithmetic and copies ran while one was open for 0% of the time, Pallas kernels for 0%

profile of v1, /device:TPU:0, one launch (start us, length us, event | category | flops | bytes accessed | tf_op | source)
XLA Modules:
  0.0 252.1 jit_solution(10015228184102862501)
XLA Ops:
  6.5 0.0 copy-start.1
  6.5 0.0 all-gather.2.cloned.1.call-start
  6.5 0.8 broadcast_in_dim_reshape_squeeze.4
  7.3 0.1 select_reduce_fusion.1
  7.4 0.7 convert_element_type.19
  8.1 0.1 select_reduce_fusion.2
  8.3 0.1 convert_element_type.20
  8.3 0.6 pad_add_fusion.places
  8.9 0.6 scatter.4.mask_ref
  9.5 2.9 %shard_map.46 = f32[1544,128]{1,0:T(8,128)} custom-call(s32[2,12]{1,0:T(2,128)} %pad_add_fusion.places, f32[8,128]{1,0:T(8,128)} %scatter.4.mask_ref, f32[512,1024]{1,0:T(8,128)} %bitcast.29), custom_call_target="tpu_custom_call" | custom-call | tf_op jit(solution)/shard_map/pallas_call | solution.py:160
  12.4 1.8 collective-permute-start
  14.2 0.0 collective-permute-done
  14.2 0.0 copy-start
  14.2 0.9 copy-done
  15.1 0.0 all-gather.2.cloned.1.call-update
  15.1 0.0 copy-done.1
  15.1 0.1 copy.11
  15.2 0.1 broadcast_in_dim.72
  15.3 0.8 copy.15
  16.2 122.4 %all-gather.2.cloned.1.call-done.a_ref = f32[24704,128]{1,0:T(8,128)} async-done(((f32[1544,128]{1,0:T(8,128)}), f32[24704,128]{1,0:T(8,128)}) %all-gather.2.cloned.1.call-update) | async-done | bytes 12648464 | tf_op jit(solution)/shard_map/all_gather | solution.py:276
  138.5 0.8 slice.20
  139.4 0.1 select_reduce_fusion
  139.5 0.1 gt.25
  139.6 0.1 mul.21
  139.7 0.1 select_bitcast_fusion
  139.8 0.2 copy.10
  140.0 0.7 reshape.157.table
  140.7 49.1 %shard_map.47 = (f32[512,1024]{1,0:T(8,128)}, f32[512,1024]{1,0:T(8,128)}) custom-call(s32[512]{0:T(512)} %reshape.157.table, f32[64,1024]{1,0:T(8,128)} %bitcast.30, f32[24704,128]{1,0:T(8,128)} %all-gather.2.cloned.1.call-done.a_ref, f32[8192,1024]{1,0:T(8,128)} %b_ref.1), custom_call_target="tpu_custom_call" | custom-call | tf_op jit(solution)/shard_map/pallas_call | solution.py:245
  189.9 5.8 %collective-permute-start.1 = (f32[512,1024]{1,0:T(8,128)}, f32[512,1024]{1,0:T(8,128)S(1)}, u32[]{:S(2)}, u32[]{:S(2)}) collective-permute-start(f32[512,1024]{1,0:T(8,128)} %get-tuple-element.20), channel_id=1, source_target_pairs={{0,16},{16,0},{1,17},{17,1},{2,18},{18,2},{3,19},{19,3},{4,20},{20... | collective-permute-start | bytes 6291464 | tf_op jit(solution)/shard_map/ppermute | solution.py:302
  195.7 46.3 %collective-permute-done.1 = f32[512,1024]{1,0:T(8,128)S(1)} collective-permute-done((f32[512,1024]{1,0:T(8,128)}, f32[512,1024]{1,0:T(8,128)S(1)}, u32[]{:S(2)}, u32[]{:S(2)}) %collective-permute-start.1) | collective-permute-done | bytes 2097184 | tf_op jit(solution)/shard_map/ppermute | solution.py:302
  241.9 3.3 %add.42 = f32[512,1024]{1,0:T(8,128)} add(f32[512,1024]{1,0:T(8,128)} %get-tuple-element.19, f32[512,1024]{1,0:T(8,128)S(1)} %collective-permute-done.1) | non-fusion elementwise | flops 524288 | bytes 6291456 | tf_op jit(solution)/shard_map/add | solution.py:302
  (8 shorter events, 0.1 us)
Async XLA Ops:
  6.5 8.6 %copy-start.1 = (s32[64,8]{0,1:T(8,128)S(1)}, s32[64,8]{0,1:T(8,128)}, u32[]{:S(2)}) copy-start(s32[64,8]{0,1:T(8,128)} %param.9) | copy-start | bytes 6148
  6.5 132.0 %all-gather.2.cloned.1.call-start = ((), (), s32[]{:S(2)}) async-start(), calls=%async_computation | async-start | bytes 13438976 | tf_op jit(solution)/shard_map/all_gather | solution.py:276
  12.4 1.8 collective-permute-start
  14.2 0.9 copy-start
  189.9 52.1 %collective-permute-start.1 = (f32[512,1024]{1,0:T(8,128)}, f32[512,1024]{1,0:T(8,128)S(1)}, u32[]{:S(2)}, u32[]{:S(2)}) collective-permute-start(f32[512,1024]{1,0:T(8,128)} %get-tuple-element.20), channel_id=1, source_target_pairs={{0,16},{16,0},{1,17},{17,1},{2,18},{18,2},{3,19},{19,3},{4,20},{20... | collective-permute-start | bytes 6291464 | tf_op jit(solution)/shard_map/ppermute | solution.py:302
Sparse Core Ops, SparseCore 0:
  15.2 123.2 all-gather.1

commit v2 on v1

--- a/solution.py
+++ b/solution.py
@@ -122,6 +122,7 @@
 
 
 CHUNK = 2
+PIECES = 2
 DEPTH = 4
 MASK_ROWS = 8
 
@@ -177,19 +178,29 @@
 
 
 def product_kernel(
-    block_size, all_rows, k_run, table, scale_ref, a_ref, b_ref, theirs_ref, mine_ref,
-    total, tile, high_ref, low_ref, offset_of, row_of, sems
+    block_size, row_blocks, first_column, table, base_ref, scale_ref, a_ref, b_ref, total,
+    blocks, tile, high_ref, low_ref, offset_of, row_of, sems, a_sem
 ):
+    k_run, width = scale_ref.shape
+
     def fetch(k):
         slot = lax.rem(k, DEPTH)
         row = pl.multiple_of(k * block_size, block_size)
         return pltpu.make_async_copy(
-            b_ref.at[pl.ds(row, block_size), :], tile.at[slot], sems.at[slot]
+            b_ref.at[pl.ds(row, block_size), pl.ds(first_column, width)],
+            tile.at[slot],
+            sems.at[slot],
         )
 
+    start_row = pl.multiple_of(base_ref[0], MASK_ROWS)
+    whole = pltpu.make_async_copy(
+        a_ref.at[pl.ds(start_row, blocks.shape[0]), :], blocks, a_sem
+    )
     for k in range(DEPTH - 1):
         fetch(k).start()
+    whole.start()
     total[...] = jnp.zeros_like(total)
+    whole.wait()
 
     @pl.loop(0, k_run)
     def step(k):
@@ -198,14 +209,11 @@
             fetch(k + DEPTH - 1).start()
 
         count = jnp.int32(0)
-        for m in range(all_rows):
-            offset = table[k * all_rows + m]
+        for m in range(row_blocks):
+            offset = table[k * row_blocks + m]
             offset_of[count] = offset
             row_of[count] = m
             count = count + (offset >= 0).astype(jnp.int32)
-        for extra in range(CHUNK - 1):
-            offset_of[count + extra] = 0
-            row_of[count + extra] = all_rows
         fetch(k).wait()
 
         @pl.when(count > 0)
@@ -217,52 +225,59 @@
             low_ref[pl.ds(0, block_size), :] = low
             low_ref[pl.ds(block_size, block_size), :] = low
 
-            @pl.loop(0, (count + CHUNK - 1) // CHUNK)
-            def chunk(c):
+            def left_of(places):
                 pieces = []
-                for i in range(CHUNK):
-                    start = pl.multiple_of(offset_of[c * CHUNK + i], MASK_ROWS)
-                    a_high, a_low = split(a_ref[pl.ds(start, block_size), :])
+                for place in places:
+                    start = pl.multiple_of(offset_of[place], MASK_ROWS)
+                    a_high, a_low = split(blocks[pl.ds(start, block_size), :])
                     pieces.append(jnp.concatenate([a_high, a_low], axis=1))
-                left = jnp.concatenate(pieces, axis=0)
+                return jnp.concatenate(pieces, axis=0)
+
+            def add(places):
+                left = left_of(places)
                 part = jnp.dot(left, high_ref[...], preferred_element_type=jnp.float32)
                 part = part + jnp.dot(left, low_ref[...], preferred_element_type=jnp.float32)
-                for i in range(CHUNK):
-                    row = pl.multiple_of(row_of[c * CHUNK + i] * block_size, block_size)
+                for i, place in enumerate(places):
+                    row = pl.multiple_of(row_of[place] * block_size, block_size)
                     total[pl.ds(row, block_size), :] += part[i * block_size:(i + 1) * block_size]
 
-    half = theirs_ref.shape[0]
-    theirs_ref[...] = total[pl.ds(0, half), :]
-    mine_ref[...] = total[pl.ds(half, half), :]
-
-
-def multiply(table, scale, gathered, b_local, block_size, all_rows):
-    k_size, width = b_local.shape
-    k_run = k_size // block_size
-    half = all_rows // 2 * block_size
-    result = jax.ShapeDtypeStruct((half, width), jnp.float32)
+            @pl.loop(0, count // CHUNK)
+            def chunk(c):
+                add([c * CHUNK + i for i in range(CHUNK)])
+
+            @pl.when(count % CHUNK == 1)
+            def last():
+                add([count - 1])
+
+
+def multiply(table, base, scale, gathered, b_local, block_size, row_blocks, first_column, width):
+    k_run = b_local.shape[0] // block_size
     vmem = pl.BlockSpec(memory_space=pltpu.VMEM)
+    smem = pl.BlockSpec(memory_space=pltpu.SMEM)
+    hbm = pl.BlockSpec(memory_space=pl.ANY)
+    part = scale[:, first_column:first_column + width]
     return pl.pallas_call(
-        functools.partial(product_kernel, block_size, all_rows, k_run),
-        out_shape=(result, result),
-        in_specs=[
-            pl.BlockSpec(memory_space=pltpu.SMEM),
-            vmem,
-            vmem,
-            pl.BlockSpec(memory_space=pl.ANY),
-        ],
-        out_specs=(vmem, vmem),
+        functools.partial(product_kernel, block_size, row_blocks, first_column),
+        out_shape=jax.ShapeDtypeStruct((row_blocks * block_size, width), jnp.float32),
+        in_specs=[smem, smem, vmem, hbm, hbm],
+        out_specs=vmem,
         scratch_shapes=[
-            pltpu.VMEM(((all_rows + 1) * block_size, width), jnp.float32),
+            pltpu.VMEM((gathered.shape[0] // 2, block_size), jnp.float32),
             pltpu.VMEM((DEPTH, block_size, width), jnp.float32),
             pltpu.VMEM((2 * block_size, width), jnp.bfloat16),
             pltpu.VMEM((2 * block_size, width), jnp.bfloat16),
-            pltpu.SMEM((all_rows + CHUNK,), jnp.int32),
-            pltpu.SMEM((all_rows + CHUNK,), jnp.int32),
+            pltpu.SMEM((row_blocks + CHUNK,), jnp.int32),
+            pltpu.SMEM((row_blocks + CHUNK,), jnp.int32),
             pltpu.SemaphoreType.DMA((DEPTH,)),
+            pltpu.SemaphoreType.DMA,
         ],
-        compiler_params=pltpu.CompilerParams(vmem_limit_bytes=60 * 1024 * 1024),
-    )(table, scale, gathered, b_local)
+        compiler_params=pltpu.CompilerParams(vmem_limit_bytes=56 * 1024 * 1024),
+        cost_estimate=pl.CostEstimate(
+            flops=4 * k_run * row_blocks * block_size * block_size * width,
+            bytes_accessed=4 * k_run * block_size * width,
+            transcendentals=0,
+        ),
+    )(table, base, part, gathered, b_local)
 
 
 def gather_a(payload, cols_per_row):
@@ -282,7 +297,6 @@
     layer_count, row_count = lax.axis_size("layer"), lax.axis_size("row")
     cols_per_row = lax.axis_size("col") // row_count
     capacity = max(2, row_blocks * q_blocks * 3 // 8)
-    all_rows = row_blocks * row_count
     payload = pack_a(a_cyclic[0], a_mask[0], block_size, capacity)
     gathered = gather_a(payload, cols_per_row)
     spots = row_blocks * q_blocks
@@ -292,14 +306,29 @@
     order = jnp.arange(spots, dtype=jnp.int32)
     earlier = order[None, :] < order[:, None]
     rank = jnp.sum(jnp.where(earlier[None], mask[:, None, :], 0.0), axis=2).astype(jnp.int32)
-    first = jnp.arange(sources, dtype=jnp.int32)[:, None] * stride
+    per_row = sources // row_count
+    first = (jnp.arange(sources, dtype=jnp.int32)[:, None] % per_row) * stride
     offset = jnp.where(mask > 0, first + rank * block_size, -1)
     offset = offset.reshape(row_count, cols_per_row, layer_count, row_blocks, q_blocks)
-    offset = offset.transpose(1, 4, 2, 0, 3)
-    offset = jnp.where(lax.axis_index("row") == 0, offset[:, :, :, ::-1], offset)
+    offset = offset.transpose(0, 1, 4, 2, 3).reshape(row_count, -1)
     scale = jnp.repeat(b_mask.astype(jnp.float32), block_size, axis=1)
-    theirs, mine = multiply(offset.reshape(-1), scale, gathered, b_dense, block_size, all_rows)
-    return mine + lax.ppermute(theirs, "row", [(0, 1), (1, 0)])
+    width = b_dense.shape[1]
+    me = lax.axis_index("row")
+
+    def rows_of(row, first_column, columns):
+        base = (row * per_row * stride).astype(jnp.int32).reshape(1)
+        table = jnp.where(row == 0, offset[0], offset[1])
+        return multiply(
+            table, base, scale, gathered, b_dense, block_size, row_blocks, first_column, columns
+        )
+
+    piece = width // PIECES
+    received = []
+    for i in range(PIECES):
+        theirs = rows_of(1 - me, i * piece, piece)
+        received.append(lax.ppermute(theirs, "row", [(0, 1), (1, 0)]))
+    mine = rows_of(me, 0, width)
+    return mine + jnp.concatenate(received, axis=1)
 
 
 def solution(mesh):

time: 253 us -> 243 us (0.960)
  waiting for transfers between devices: 169 us -> 122 us
  Pallas kernels: 52 us -> 86.6 us
    ppermute x1 -> x2, waiting for transfers between devices: 46.3 us -> 0.01 us  [on_pair_device(): received.append(lax.ppermute(theirs, 'row', [(0, 1), (1, 0)]))]
    pallas_call x1 -> x3, Pallas kernels: 49.1 us -> 83.8 us  [multiply(): pl.pallas_call(functools.partial(product_kernel, block_size, row_blocks,...]
    ppermute x1 -> x2, starting transfers between devices: 5.8 us -> 5.02 us  [on_pair_device(): received.append(lax.ppermute(theirs, 'row', [(0, 1), (1, 0)]))]
  transfers between devices with their start and end apart: 3 -> 4, of which waited for: 2 -> 1; matrix products, arithmetic and copies ran while one was open for 0% -> 0% of each run, Pallas kernels for 0% -> 24%
where the time goes in v2:
time: 243 us; the launch traced here: 241 us
  waiting for transfers between devices  122 us (50%)
  Pallas kernels  86.6 us (36%)
  between operations  13.6 us (6%)
  starting transfers between devices  6.82 us (3%)
  local copies, waits for them, and re-layouts  6.02 us (2%)
  other arithmetic  5.14 us (2%)
    all_gather x1, waiting for transfers between devices, gather_a(): return lax.all_gather(moved, ('col', 'layer'), axis=0, tiled=True)  122 us
    pallas_call x3, Pallas kernels, multiply(): pl.pallas_call(functools.partial(product_kernel, block_size, row_blocks,...  83.8 us
    ppermute x2, starting transfers between devices, on_pair_device(): received.append(lax.ppermute(theirs, 'row', [(0, 1), (1, 0)]))  5.02 us
  transfers between devices with their start and end apart: 4, of which 1 were waited for; matrix products, arithmetic and copies ran while one was open for 0% of the time, Pallas kernels for 24%

profile of v2, /device:TPU:0, one launch (start us, length us, event | category | flops | bytes accessed | tf_op | source)
XLA Modules:
  0.0 240.6 jit_solution(7515224471004383865)
XLA Ops:
  6.5 0.0 copy-start.2
  6.5 0.0 all-gather.2.cloned.1.call-start
  6.5 0.8 broadcast_in_dim_reshape_squeeze.4
  7.3 0.1 select_reduce_fusion.1
  7.4 0.7 convert_element_type.19
  8.1 0.1 select_reduce_fusion.2
  8.3 0.1 convert_element_type.20
  8.3 0.6 pad_add_fusion.places
  8.9 0.6 scatter.4.mask_ref
  9.5 2.8 %shard_map.46 = f32[1544,128]{1,0:T(8,128)} custom-call(s32[2,12]{1,0:T(2,128)} %pad_add_fusion.places, f32[8,128]{1,0:T(8,128)} %scatter.4.mask_ref, f32[512,1024]{1,0:T(8,128)} %bitcast.31), custom_call_target="tpu_custom_call" | custom-call | tf_op jit(solution)/shard_map/pallas_call | solution.py:161
  12.3 1.8 collective-permute-start
  14.1 0.0 collective-permute-done
  14.1 0.0 copy-start.1
  14.1 0.9 copy-done.1
  15.0 0.0 all-gather.2.cloned.1.call-update
  15.1 0.0 copy-done.2
  15.1 0.1 copy.12
  15.2 0.1 broadcast_in_dim.72
  15.3 0.1 copy.17
  15.4 0.0 copy-start
  15.4 0.8 fusion.2
  16.2 122.4 %all-gather.2.cloned.1.call-done.a_ref = f32[24704,128]{1,0:T(8,128)} async-done(((f32[1544,128]{1,0:T(8,128)}), f32[24704,128]{1,0:T(8,128)}) %all-gather.2.cloned.1.call-update) | async-done | bytes 12648464 | tf_op jit(solution)/shard_map/all_gather | solution.py:291
  138.5 0.8 slice.42
  139.4 0.1 gt.25
  139.5 0.1 select_reduce_fusion
  139.6 0.1 mul.31
  139.7 0.1 select_bitcast_fusion
  139.8 0.1 copy.11
  140.0 0.7 select_n.83.table
  140.7 0.1 copy.13
  140.8 0.7 select_n.86.table
  141.5 25.0 %shard_map.49 = f32[512,512]{1,0:T(8,128)} custom-call(s32[256]{0:T(256)} %select_n.86.table, s32[1]{0:T(128)} %bitcast.6.base_ref, f32[64,512]{1,0:T(8,128)} %get-tuple-element.18.scale_ref, f32[24704,128]{1,0:T(8,128)} %all-gather.2.cloned.1.call-done.a_ref, f32[8192,1024]{1,0:T(8,128)} %b_ref.5), custom_call_target="tpu_custom_call" | custom-call | flops 8589934592 | bytes 16777216 | tf_op jit(solution)/shard_map/pallas_call | solution.py:259
  166.5 0.0 copy-done
  166.5 3.2 %collective-permute-start.2 = (f32[512,512]{1,0:T(8,128)}, f32[512,512]{1,0:T(8,128)S(1)}, u32[]{:S(2)}, u32[]{:S(2)}) collective-permute-start(f32[512,512]{1,0:T(8,128)} %shard_map.49), channel_id=1, source_target_pairs={{0,16},{16,0},{1,17},{17,1},{2,18},{18,2},{3,19},{19,3},{4,20},{20... | collective-permute-start | bytes 3145736 | tf_op jit(solution)/shard_map/ppermute | solution.py:329
  169.8 25.0 %shard_map.48 = f32[512,512]{1,0:T(8,128)} custom-call(s32[256]{0:T(256)} %select_n.86.table, s32[1]{0:T(128)} %bitcast.6.base_ref, f32[64,512]{1,0:T(8,128)} %get-tuple-element.17.scale_ref, f32[24704,128]{1,0:T(8,128)} %all-gather.2.cloned.1.call-done.a_ref, f32[8192,1024]{1,0:T(8,128)} %b_ref.5), custom_call_target="tpu_custom_call" | custom-call | flops 8589934592 | bytes 16777216 | tf_op jit(solution)/shard_map/pallas_call | solution.py:259
  194.8 1.8 collective-permute-start.1
  196.6 33.7 %shard_map.47 = f32[512,1024]{1,0:T(8,128)} custom-call(s32[256]{0:T(256)} %select_n.83.table, s32[1]{0:T(128)} %bitcast.5.base_ref, f32[64,1024]{1,0:T(8,128)} %bitcast.33, f32[24704,128]{1,0:T(8,128)} %all-gather.2.cloned.1.call-done.a_ref, f32[8192,1024]{1,0:T(8,128)} %b_ref.5), custom_call_target="tpu_custom_call" | custom-call | flops 17179869184 | bytes 33554432 | tf_op jit(solution)/shard_map/pallas_call | solution.py:259
  230.3 0.0 collective-permute-done.2
  230.3 0.0 collective-permute-done.1
  230.3 3.4 %maximum_add_fusion = f32[512,1024]{1,0:T(8,128)} fusion(f32[512,1024]{1,0:T(8,128)} %shard_map.47, f32[512,512]{1,0:T(8,128)S(1)} %collective-permute-done.2, f32[512,512]{1,0:T(8,128)S(1)} %collective-permute-done.1), kind=kLoop, calls=%fused_computation | loop fusion | flops 1048576 | bytes 6291456 | tf_op jit(solution)/shard_map/add | solution.py:331
  (8 shorter events, 0.1 us)
Async XLA Ops:
  6.5 8.5 %copy-start.2 = (s32[64,8]{0,1:T(8,128)S(1)}, s32[64,8]{0,1:T(8,128)}, u32[]{:S(2)}) copy-start(s32[64,8]{0,1:T(8,128)} %param.9) | copy-start | bytes 6148
  6.5 132.0 %all-gather.2.cloned.1.call-start = ((), (), s32[]{:S(2)}) async-start(), calls=%async_computation | async-start | bytes 13438976 | tf_op jit(solution)/shard_map/all_gather | solution.py:291
  12.3 1.8 collective-permute-start
  14.1 0.9 copy-start.1
  15.4 151.2 %copy-start = (f32[8,8,8,128]{3,1,2,0:T(8,128)}, f32[8,8,8,128]{3,1,2,0:T(8,128)S(1)}, u32[]{:S(2)}) copy-start(f32[8,8,8,128]{3,1,2,0:T(8,128)S(1)} %copy.17) | copy-start | bytes 786436
  166.5 63.8 %collective-permute-start.2 = (f32[512,512]{1,0:T(8,128)}, f32[512,512]{1,0:T(8,128)S(1)}, u32[]{:S(2)}, u32[]{:S(2)}) collective-permute-start(f32[512,512]{1,0:T(8,128)} %shard_map.49), channel_id=1, source_target_pairs={{0,16},{16,0},{1,17},{17,1},{2,18},{18,2},{3,19},{19,3},{4,20},{20... | collective-permute-start | bytes 3145736 | tf_op jit(solution)/shard_map/ppermute | solution.py:329
  194.8 35.5 %collective-permute-start.1 = (f32[512,512]{1,0:T(8,128)}, f32[512,512]{1,0:T(8,128)S(1)}, u32[]{:S(2)}, u32[]{:S(2)}) collective-permute-start(f32[512,512]{1,0:T(8,128)} %shard_map.48), channel_id=1, source_target_pairs={{0,16},{16,0},{1,17},{17,1},{2,18},{18,2},{3,19},{19,3},{4,20},{20... | collective-permute-start | bytes 3145736 | tf_op jit(solution)/shard_map/ppermute | solution.py:329
Sparse Core Ops, SparseCore 0:
  15.2 123.3 all-gather.1
